TPU v7x, 32 devices: a whole 2x2x4 slice. The times are simulated.
32 devices in a mesh: gx: 2 (over y), gy: 16 (over z, x, core).
Axes of the slice: x: 2, y: 2, z: 4, core: 2. Of those that a mesh axis runs over, the one named last changes fastest.
Arguments:
- basis_mats: float32 [12, 275, 275], replicated, may hold values from -8 to 8.5, as said below
- coeffs: float32 [512, 12], P(('gx', 'gy')), may hold values from 0.5 to 2
- element_loads: float32 [512, 275], P(('gx', 'gy')), may hold values from -18 to 18
- elem_faces: int32 [512, 6], P(('gx', 'gy')), may hold values from 0 to 71, as said below
- orient_codes: int32 [512, 6], P(('gx', 'gy')), may hold values from 0 to 7
- shared_owned: int32 [32, 2, 4], P(('gx', 'gy')), may hold values from 0 to 63, as said below
- shared_remote: int32 [32, 2, 4], P(('gx', 'gy')), may hold values from 0 to 7, as said below
- lower_peers: int32 [32, 2], P(('gx', 'gy')), may hold values from 0 to 31, as said below
- upper_peers: int32 [32, 2], P(('gx', 'gy')), may hold values from 0 to 31, as said below
Outputs:
- trace: float32 [25, 2048], P(None, ('gx', 'gy'))
- residual: float32 [25, 2048], P(None, ('gx', 'gy'))
Inputs may be any that keep to these rules, and one draw needn't show every extreme that they name: `basis_mats`: each matrix is symmetric with every eigenvalue at least 0.5. `elem_faces`: an entry below 64 is a face slot that the element's device owns; an entry 64 + r is that device's remote slot r. Every owned slot of a device is named by one or two of its element faces, every remote slot by exactly one. `shared_owned`: row (d, i) lists 4 distinct owned slots of device d, in message order, that device lower_peers[d, i] uses; the two rows of a device are disjoint. `shared_remote`: row (d, i) lists remote slots of device d in message order: its k-th entry is the face that device upper_peers[d, i] lists k-th in its row i of shared_owned. The two rows of a device together hold each of its 8 remote slots once. upper_peers[lower_peers[d, i], i] = d for every device d and i; the two entries of a row differ. Peers are arbitrary device numbers. lower_peers[upper_peers[d, i], i] = d for every device d and i; the two entries of a row differ; each column is a permutation of the devices. Peers are arbitrary device numbers.
All inputs are finite; a program needn't handle non-finite values.
Results may differ from a plain program's by a relative error of at most 0.0003.
Values sent between devices are 32-bit elements; how exact they have to be, the bound alone decides.
A program may use at most 128 MiB of HBM per device.

v0:
```python
import math
import jax
import jax.numpy as jnp
import numpy as np
from jax import lax
from jax.sharding import PartitionSpec as P

SIDE = 5
FACE_DOFS = 25
CELL_DOFS = 125
TRACE_DOFS = 150
ITERS = 4
FACE_DEV = 64
SHARED = 4
REMOTE = 8
full_precision = lax.Precision.HIGHEST


def orient_table():
    edge_nodes = SIDE
    codes_table = np.zeros((8, edge_nodes * edge_nodes), np.int32)
    for code_index in range(8):
        for first_axis in range(edge_nodes):
            for second_axis in range(edge_nodes):
                if code_index & 1:
                    first_new, second_new = (second_axis, first_axis)
                else:
                    first_new, second_new = (first_axis, second_axis)
                if code_index & 2:
                    first_new = edge_nodes - 1 - first_new
                if code_index & 4:
                    second_new = edge_nodes - 1 - second_new
                codes_table[code_index, first_axis * edge_nodes + second_axis] = (
                    first_new * edge_nodes + second_new
                )
    return codes_table


def permute_mats():
    codes_table = orient_table()
    matrices = np.zeros((8, FACE_DOFS, FACE_DOFS), np.float32)
    for code_index in range(8):
        for position in range(FACE_DOFS):
            matrices[code_index, position, codes_table[code_index, position]] = 1.0
    return matrices


def condense(coeffs, element_loads, basis_mats):
    element_mats = jnp.einsum("ek,kab->eab", coeffs, basis_mats, precision=full_precision)
    inner_block = element_mats[:, :CELL_DOFS, :CELL_DOFS]
    coupling = element_mats[:, :CELL_DOFS, CELL_DOFS:]
    outer_block = element_mats[:, CELL_DOFS:, CELL_DOFS:]
    factor = jnp.linalg.cholesky(inner_block)
    solved = jax.scipy.linalg.solve_triangular(factor, coupling, lower=True)
    source = jax.scipy.linalg.solve_triangular(
        factor, element_loads[:, :CELL_DOFS, None], lower=True
    )[:, :, 0]
    schur_part = outer_block - jnp.einsum("eib,eic->ebc", solved, solved, precision=full_precision)
    load_trace = element_loads[:, CELL_DOFS:] - jnp.einsum(
        "eib,ei->eb", solved, source, precision=full_precision
    )
    return (schur_part, load_trace)


def condense_blocks(coeffs, element_loads, basis_mats):
    elem_count = coeffs.shape[0]
    block_rows = math.gcd(elem_count, 16)
    grouped = (
        coeffs.reshape(-1, block_rows, coeffs.shape[1]),
        element_loads.reshape(-1, block_rows, element_loads.shape[1]),
    )
    schur_part, load_trace = lax.map(
        lambda pieces: condense(pieces[0], pieces[1], basis_mats), grouped
    )
    return (
        schur_part.reshape(elem_count, TRACE_DOFS, TRACE_DOFS),
        load_trace.reshape(elem_count, TRACE_DOFS),
    )


def pick_columns(fields, columns):
    picked = fields[:, :, columns]
    return jnp.moveaxis(picked, 2, 0).reshape(2, -1)


def place_rows(fields, columns, arrived):
    shaped = jnp.moveaxis(arrived.reshape(2, fields.shape[0], FACE_DOFS, SHARED), 0, 2)
    return fields.at[:, :, columns].add(shaped)


def owned_dot(first, second):
    return jnp.sum(first * second)


def on_device(
    basis_mats,
    coeffs,
    element_loads,
    elem_faces,
    orient_codes,
    shared_owned,
    shared_remote,
    lower_peers,
    upper_peers,
):
    elem_count = coeffs.shape[0]
    extent = FACE_DEV + REMOTE
    size_outer = lax.axis_size("gx")
    size_inner = lax.axis_size("gy")
    devices = size_outer * size_inner
    schur_blocks, load_trace = condense_blocks(coeffs, element_loads, basis_mats)
    choose = (orient_codes[:, :, None] == jnp.arange(8, dtype=jnp.int32)[None, None, :]).astype(
        jnp.float32
    )
    permute = jnp.einsum(
        "ejo,oqp->ejqp", choose, jnp.asarray(permute_mats()), precision=full_precision
    )
    incidence = (
        elem_faces.reshape(-1)[:, None] == jnp.arange(extent, dtype=jnp.int32)[None, :]
    ).astype(jnp.float32)
    owned_lists = shared_owned[0]
    remote_lists = FACE_DEV + shared_remote[0]
    lower_ids = lower_peers[0]
    upper_ids = upper_peers[0]

    def spread(field_values):
        gathered = jnp.dot(incidence, field_values.T, precision=full_precision).reshape(
            elem_count, 6, FACE_DOFS
        )
        return jnp.einsum("ejqp,ejp->ejq", permute, gathered, precision=full_precision).reshape(
            elem_count, TRACE_DOFS
        )

    def collect(element_values):
        shaped = element_values.reshape(elem_count, 6, FACE_DOFS)
        placed = jnp.einsum("ejqp,ejq->ejp", permute, shaped, precision=full_precision)
        return jnp.dot(
            placed.reshape(elem_count * 6, FACE_DOFS).T, incidence, precision=full_precision
        )

    def apply_blocks(field_values):
        return collect(
            jnp.einsum("ekl,el->ek", schur_blocks, spread(field_values), precision=full_precision)
        )

    fields = jnp.stack([collect(load_trace), collect(jnp.diagonal(schur_blocks, axis1=1, axis2=2))])

    def upward_bucket(partial_value):
        outgoing = pick_columns(partial_value, remote_lists)
        bucket = jnp.zeros((devices, outgoing.shape[1]), jnp.float32).at[upper_ids].set(outgoing)
        return bucket.reshape(size_outer, size_inner, -1)

    def upward_settle(partial_value, arrived):
        incoming = arrived.reshape(devices, -1)[lower_ids]
        return place_rows(partial_value[:, :, :FACE_DEV], owned_lists, incoming)

    def downward_bucket(values):
        outgoing = pick_columns(values[None], owned_lists)
        bucket = jnp.zeros((devices, outgoing.shape[1]), jnp.float32).at[lower_ids].set(outgoing)
        return bucket.reshape(size_outer, size_inner, -1)

    def downward_settle(values, arrived):
        incoming = arrived.reshape(devices, -1)[upper_ids]
        remote = place_rows(
            jnp.zeros((1, FACE_DOFS, REMOTE), jnp.float32), shared_remote[0], incoming
        )
        return jnp.concatenate([values, remote[0]], axis=1)

    arrived = lax.all_to_all(
        lax.all_to_all(upward_bucket(fields), "gx", split_axis=0, concat_axis=0, tiled=True),
        "gy",
        split_axis=1,
        concat_axis=1,
        tiled=True,
    )
    settled = upward_settle(fields, arrived)

    def operate(values):
        fetched = lax.all_to_all(
            lax.all_to_all(downward_bucket(values), "gx", split_axis=0, concat_axis=0, tiled=True),
            "gy",
            split_axis=1,
            concat_axis=1,
            tiled=True,
        )
        partial_value = apply_blocks(downward_settle(values, fetched))[None]
        returned = lax.all_to_all(
            lax.all_to_all(
                upward_bucket(partial_value), "gx", split_axis=0, concat_axis=0, tiled=True
            ),
            "gy",
            split_axis=1,
            concat_axis=1,
            tiled=True,
        )
        return upward_settle(partial_value, returned)[0]

    rhs_faces = settled[0]
    diag_faces = settled[1]

    def pair_total(residual, precond, mapped):
        return lax.psum((owned_dot(residual, precond), owned_dot(precond, mapped)), ("gx", "gy"))

    trace = jnp.zeros_like(rhs_faces)
    residual = rhs_faces
    precond = residual / diag_faces
    mapped = operate(precond)
    rz_now, curve_sum = pair_total(residual, precond, mapped)
    step_size = rz_now / curve_sum
    direction = precond
    direction_image = mapped
    for iteration in range(ITERS):
        trace = trace + step_size * direction
        residual = residual - step_size * direction_image
        if iteration + 1 < ITERS:
            precond = residual / diag_faces
            mapped = operate(precond)
            rz_next, curve_sum = pair_total(residual, precond, mapped)
            ratio_next = rz_next / rz_now
            step_size = rz_next / (curve_sum - ratio_next * rz_next / step_size)
            direction = precond + ratio_next * direction
            direction_image = mapped + ratio_next * direction_image
            rz_now = rz_next
    return (trace, residual)


def solution(mesh):
    placed = (
        P(),
        P(("gx", "gy"), None),
        P(("gx", "gy"), None),
        P(("gx", "gy"), None),
        P(("gx", "gy"), None),
        P(("gx", "gy"), None, None),
        P(("gx", "gy"), None, None),
        P(("gx", "gy"), None),
        P(("gx", "gy"), None),
    )
    return jax.shard_map(
        on_device,
        mesh=mesh,
        in_specs=placed,
        out_specs=(P(None, ("gx", "gy")), P(None, ("gx", "gy"))),
        check_vma=False,
    )
```

profile of v0, /device:TPU:0, one launch (start us, length us, event | category | flops | bytes accessed | tf_op | source)
XLA Modules:
  0.0 803.4 jit_solution(2315458276905869473)
XLA Ops:
  1.3 9.7 %fusion = f32[16,275,275]{2,0,1:T(8,128)S(1)} fusion(f32[12,275,275]{2,1,0:T(8,128)} %param.10, f32[16,12]{1,0:T(8,128)S(1)} %copy-done), kind=kOutput, calls=%fused_computation.37 | convolution fusion | flops 174240000 | bytes 8470768 | tf_op jit(solution)/shard_map/while/body/eval_jaxpr/ek,kab->eab/dot_general | solution.py:49
  16.7 183.1 %custom-call.13 = f32[16,125,125]{2,1,0:T(8,128)S(1)} custom-call(f32[16,125,125]{2,1,0:T(8,128)S(1)} %fusion.20), custom_call_target="Cholesky" | custom-call | tf_op jit(solution)/shard_map/while/body/eval_jaxpr/jit(cholesky)/cholesky | solution.py:53
  200.3 154.0 %custom-call.14 = f32[16,1,125,125]{2,3,1,0:T(8,128)S(1)} custom-call(f32[16,1,125,125]{3,2,1,0:T(8,128)S(1)} %select_bitcast_fusion), custom_call_target="InvertDiagBlocksLowerTriangular" | custom-call | tf_op jit(solution)/shard_map/while/body/eval_jaxpr/jit(_solve_triangular)/vmap()/triangular_solve | solution.py:54
  354.3 5.9 fusion.10
  377.6 6.7 copy.285
  384.2 6.0 gather_fusion
  397.1 4.3 all-to-all-start
  405.9 6.4 all-to-all-start.1
  412.4 6.5 all-to-all-done.1
  422.0 6.2 all_to_all.90
  432.5 6.3 all-to-all-done.3
  440.7 4.1 fusion.16
  454.3 6.2 all_to_all.91
  464.7 6.4 all-to-all-done.5
  473.1 38.3 %all-reduce.3 = (f32[]{:T(128)}, f32[]{:T(128)}) all-reduce(f32[]{:T(128)} %get-tuple-element.39, f32[]{:T(128)} %get-tuple-element.38), channel_id=1, replica_groups=mesh['gx'=2,'gy'=16] {'gx','gy'}, use_global_device_ids=true, to_apply=%region_5.6 | all-reduce | flops 2 | bytes 16 | tf_op jit(solution)/shard_map/psum | solution.py:202
  514.2 7.4 all_to_all.92
  525.8 6.4 all-to-all-done.7
  534.3 4.1 fusion.14
  548.0 6.2 all_to_all.93
  558.4 6.4 all-to-all-done.9
  566.8 38.3 %all-reduce.2 = (f32[]{:T(128)}, f32[]{:T(128)}) all-reduce(f32[]{:T(128)} %get-tuple-element.37, f32[]{:T(128)} %get-tuple-element.36), channel_id=1, replica_groups=mesh['gx'=2,'gy'=16] {'gx','gy'}, use_global_device_ids=true, to_apply=%region_13.14 | all-reduce | flops 2 | bytes 16 | tf_op jit(solution)/shard_map/psum | solution.py:202
  611.0 7.4 all_to_all.94
  622.7 6.4 all-to-all-done.11
  644.6 6.2 all_to_all.95
  655.0 6.4 all-to-all-done.13
  663.4 38.3 %all-reduce.1 = (f32[]{:T(128)}, f32[]{:T(128)}) all-reduce(f32[]{:T(128)} %get-tuple-element.35, f32[]{:T(128)} %get-tuple-element.34), channel_id=1, replica_groups=mesh['gx'=2,'gy'=16] {'gx','gy'}, use_global_device_ids=true, to_apply=%region_21.22 | all-reduce | flops 2 | bytes 16 | tf_op jit(solution)/shard_map/psum | solution.py:202
  707.2 7.4 all_to_all.96
  718.8 6.4 all-to-all-done.15
  727.2 4.1 fusion.18
  740.8 6.2 all_to_all.97
  751.2 6.4 all-to-all-done.17
  759.7 38.4 %all-reduce = (f32[]{:T(128)}, f32[]{:T(128)}) all-reduce(f32[]{:T(128)} %get-tuple-element.33, f32[]{:T(128)} %get-tuple-element.32), channel_id=1, replica_groups=mesh['gx'=2,'gy'=16] {'gx','gy'}, use_global_device_ids=true, to_apply=%region_29.30 | all-reduce | flops 2 | bytes 16 | tf_op jit(solution)/shard_map/psum | solution.py:202
  (247 shorter events, 135.8 us)
Async XLA Ops:
  0.6 0.7 copy-start
  11.1 2.8 copy-start.2
  354.2 5.9 slice-start
  361.2 5.6 copy-start.4
  361.2 5.9 copy-start.3
  361.2 5.9 copy-start.5
  370.9 2.7 copy-start.1
  370.9 2.6 copy-start.6
  384.2 10.8 %copy-start.7 = (s32[1,2,4]{2,1,0:T(2,128)S(1)}, s32[1,2,4]{2,1,0:T(2,128)}, u32[]{:S(2)}) copy-start(s32[1,2,4]{2,1,0:T(2,128)} %param.16) | copy-start | bytes 100
  384.2 11.7 %copy-start.9 = (s32[1,2]{1,0:T(1,128)S(1)}, s32[1,2]{1,0:T(1,128)}, u32[]{:S(2)}) copy-start(s32[1,2]{1,0:T(1,128)} %param.18) | copy-start | bytes 28
  384.2 17.1 %copy-start.10 = (s32[1,2]{1,0:T(1,128)S(1)}, s32[1,2]{1,0:T(1,128)}, u32[]{:S(2)}) copy-start(s32[1,2]{1,0:T(1,128)} %param.17) | copy-start | bytes 28
  384.2 17.1 %copy-start.8 = (s32[1,2,4]{2,1,0:T(2,128)S(1)}, s32[1,2,4]{2,1,0:T(2,128)}, u32[]{:S(2)}) copy-start(s32[1,2,4]{2,1,0:T(2,128)} %param.15) | copy-start | bytes 100
  397.1 8.2 %all-to-all-start = ((f32[2,16,200]{2,1,0:T(8,128)}), f32[2,16,200]{2,1,0:T(8,128)S(1)}, u32[]{:S(2)}, u32[]{:S(2)}) async-start(f32[2,16,200]{2,1,0:T(8,128)} %bitcast.26), calls=%async_computation | async-start | bytes 65536 | tf_op jit(solution)/shard_map/all_to_all | solution.py:170
  405.9 13.0 %all-to-all-start.1 = ((f32[2,16,200]{2,0,1:T(2,128)}), f32[2,16,200]{2,0,1:T(2,128)S(1)}, u32[]{:S(2)}, u32[]{:S(2)}) async-start(f32[2,16,200]{2,0,1:T(2,128)} %copy.290), calls=%async_computation.1 | async-start | bytes 65536 | tf_op jit(solution)/shard_map/all_to_all | solution.py:169
  428.8 10.0 %all-to-all-start.3 = ((f32[2,16,100]{2,0,1:T(2,128)}), f32[2,16,100]{2,0,1:T(2,128)S(1)}, u32[]{:S(2)}, u32[]{:S(2)}) async-start(f32[2,16,100]{2,0,1:T(2,128)} %copy.298), calls=%async_computation.3 | async-start | bytes 32768 | tf_op jit(solution)/shard_map/all_to_all | solution.py:179
  461.1 10.0 %all-to-all-start.5 = ((f32[2,16,100]{2,0,1:T(2,128)}), f32[2,16,100]{2,0,1:T(2,128)S(1)}, u32[]{:S(2)}, u32[]{:S(2)}) async-start(f32[2,16,100]{2,0,1:T(2,128)} %copy.306), calls=%async_computation.5 | async-start | bytes 32768 | tf_op jit(solution)/shard_map/all_to_all | solution.py:187
  522.2 10.1 %all-to-all-start.7 = ((f32[2,16,100]{2,0,1:T(2,128)}), f32[2,16,100]{2,0,1:T(2,128)S(1)}, u32[]{:S(2)}, u32[]{:S(2)}) async-start(f32[2,16,100]{2,0,1:T(2,128)} %copy.312), calls=%async_computation.7 | async-start | bytes 32768 | tf_op jit(solution)/shard_map/all_to_all | solution.py:179
  554.8 10.0 %all-to-all-start.9 = ((f32[2,16,100]{2,0,1:T(2,128)}), f32[2,16,100]{2,0,1:T(2,128)S(1)}, u32[]{:S(2)}, u32[]{:S(2)}) async-start(f32[2,16,100]{2,0,1:T(2,128)} %copy.320), calls=%async_computation.9 | async-start | bytes 32768 | tf_op jit(solution)/shard_map/all_to_all | solution.py:187
  619.1 10.0 %all-to-all-start.11 = ((f32[2,16,100]{2,0,1:T(2,128)}), f32[2,16,100]{2,0,1:T(2,128)S(1)}, u32[]{:S(2)}, u32[]{:S(2)}) async-start(f32[2,16,100]{2,0,1:T(2,128)} %copy.326), calls=%async_computation.11 | async-start | bytes 32768 | tf_op jit(solution)/shard_map/all_to_all | solution.py:179
  651.4 10.0 %all-to-all-start.13 = ((f32[2,16,100]{2,0,1:T(2,128)}), f32[2,16,100]{2,0,1:T(2,128)S(1)}, u32[]{:S(2)}, u32[]{:S(2)}) async-start(f32[2,16,100]{2,0,1:T(2,128)} %copy.334), calls=%async_computation.13 | async-start | bytes 32768 | tf_op jit(solution)/shard_map/all_to_all | solution.py:187
  715.2 10.1 %all-to-all-start.15 = ((f32[2,16,100]{2,0,1:T(2,128)}), f32[2,16,100]{2,0,1:T(2,128)S(1)}, u32[]{:S(2)}, u32[]{:S(2)}) async-start(f32[2,16,100]{2,0,1:T(2,128)} %copy.340), calls=%async_computation.15 | async-start | bytes 32768 | tf_op jit(solution)/shard_map/all_to_all | solution.py:179
  747.6 10.0 %all-to-all-start.17 = ((f32[2,16,100]{2,0,1:T(2,128)}), f32[2,16,100]{2,0,1:T(2,128)S(1)}, u32[]{:S(2)}, u32[]{:S(2)}) async-start(f32[2,16,100]{2,0,1:T(2,128)} %copy.348), calls=%async_computation.17 | async-start | bytes 32768 | tf_op jit(solution)/shard_map/all_to_all | solution.py:187
where the time goes:
time: 814 us; the launch traced here: 803 us
  other arithmetic  352 us (43%)
  blocking collectives  207 us (25%)
  matrix products  79.3 us (10%)
  waiting for transfers between devices  61.3 us (8%)
  local copies, waits for them, and re-layouts  50.7 us (6%)
  starting transfers between devices  38.8 us (5%)
  between operations  15.2 us (2%)
    another operation x4, other arithmetic, condense(): factor = jnp.linalg.cholesky(inner_block)  183 us
    another operation x3, other arithmetic, condense(): solved = jax.scipy.linalg.solve_triangular(factor, coupling, lower=True)  154 us
    psum x4, blocking collectives, pair_total(): lax.psum((owned_dot(residual, precond), owned_dot(precond, mapped)), ('gx...  153 us
    all_to_all x4, blocking collectives, operate(): lax.all_to_all(downward_bucket(values), 'gx', split_axis=0, concat_axis=0...  28.4 us
    all_to_all x4, waiting for transfers between devices, operate(): lax.all_to_all(lax.all_to_all(downward_bucket(values), 'gx', split_axis=0...  25.5 us
    all_to_all x4, waiting for transfers between devices, operate(): lax.all_to_all(lax.all_to_all(upward_bucket(partial_value), 'gx', split_a...  25.4 us
    all_to_all x4, blocking collectives, operate(): lax.all_to_all(upward_bucket(partial_value), 'gx', split_axis=0, concat_a...  24.8 us
    dot_general x6, matrix products, collect(): jnp.einsum('ejqp,ejq->ejp', permute, shaped, precision=full_precision)  22.3 us
  transfers between devices with their start and end apart: 10, of which 10 were waited for; matrix products, arithmetic and copies ran while one was open for 0% of the time, Pallas kernels for 0%

commit v1 on v0

--- a/solution.py
+++ b/solution.py
@@ -184,15 +184,12 @@
             tiled=True,
         )
         partial_value = apply_blocks(downward_settle(values, fetched))[None]
-        returned = lax.all_to_all(
-            lax.all_to_all(
-                upward_bucket(partial_value), "gx", split_axis=0, concat_axis=0, tiled=True
-            ),
-            "gy",
-            split_axis=1,
-            concat_axis=1,
-            tiled=True,
-        )
+        own = lax.all_to_all(
+            upward_bucket(partial_value), "gx", split_axis=0, concat_axis=0, tiled=True
+        )
+        parts = jnp.split(own, lax.axis_size("gy"), axis=1)
+        received = lax.all_to_all(jnp.stack(parts), "gy", 0, 0)
+        returned = jnp.concatenate(received, axis=1)
         return upward_settle(partial_value, returned)[0]
 
     rhs_faces = settled[0]

time: 814 us -> 847 us (1.041)
  local copies, waits for them, and re-layouts: 50.7 us -> 84.3 us
    unnamed x26 -> x86, local copies, waits for them, and re-layouts: 5.37 us -> 39.1 us
where the time goes in v1:
time: 847 us; the launch traced here: 837 us
  other arithmetic  352 us (42%)
  blocking collectives  207 us (24%)
  local copies, waits for them, and re-layouts  84.3 us (10%)
  matrix products  79.3 us (9%)
  waiting for transfers between devices  61.4 us (7%)
  starting transfers between devices  38.8 us (5%)
  between operations  15.2 us (2%)
    another operation x4, other arithmetic, condense(): factor = jnp.linalg.cholesky(inner_block)  183 us
    another operation x3, other arithmetic, condense(): solved = jax.scipy.linalg.solve_triangular(factor, coupling, lower=True)  154 us
    psum x4, blocking collectives, pair_total(): lax.psum((owned_dot(residual, precond), owned_dot(precond, mapped)), ('gx...  153 us
    unnamed x86, local copies, waits for them, and re-layouts  39.1 us
    all_to_all x4, blocking collectives, operate(): lax.all_to_all(downward_bucket(values), 'gx', split_axis=0, concat_axis=0...  28.4 us
    all_to_all x4, waiting for transfers between devices, operate(): lax.all_to_all(lax.all_to_all(downward_bucket(values), 'gx', split_axis=0...  25.5 us
    all_to_all x4, waiting for transfers between devices, operate(): received = lax.all_to_all(jnp.stack(parts), 'gy', 0, 0)  25.4 us
    all_to_all x4, blocking collectives, operate(): lax.all_to_all(upward_bucket(partial_value), 'gx', split_axis=0, concat_a...  24.8 us
  transfers between devices with their start and end apart: 10, of which 10 were waited for; matrix products, arithmetic and copies ran while one was open for 0% of the time, Pallas kernels for 0%

profile of v1, /device:TPU:0, one launch (start us, length us, event | category | flops | bytes accessed | tf_op | source)
XLA Modules:
  0.0 837.2 jit_solution(12291283799245094013)
XLA Ops:
  1.3 9.7 %fusion = f32[16,275,275]{2,0,1:T(8,128)S(1)} fusion(f32[12,275,275]{2,1,0:T(8,128)} %param.10, f32[16,12]{1,0:T(8,128)S(1)} %copy-done), kind=kOutput, calls=%fused_computation.37 | convolution fusion | flops 174240000 | bytes 8470768 | tf_op jit(solution)/shard_map/while/body/eval_jaxpr/ek,kab->eab/dot_general | solution.py:49
  16.7 183.1 %custom-call.13 = f32[16,125,125]{2,1,0:T(8,128)S(1)} custom-call(f32[16,125,125]{2,1,0:T(8,128)S(1)} %fusion.20), custom_call_target="Cholesky" | custom-call | tf_op jit(solution)/shard_map/while/body/eval_jaxpr/jit(cholesky)/cholesky | solution.py:53
  200.3 154.0 %custom-call.14 = f32[16,1,125,125]{2,3,1,0:T(8,128)S(1)} custom-call(f32[16,1,125,125]{3,2,1,0:T(8,128)S(1)} %select_bitcast_fusion), custom_call_target="InvertDiagBlocksLowerTriangular" | custom-call | tf_op jit(solution)/shard_map/while/body/eval_jaxpr/jit(_solve_triangular)/vmap()/triangular_solve | solution.py:54
  354.3 5.9 fusion.10
  377.6 6.7 copy.725
  384.2 6.0 gather_fusion
  397.2 4.3 all-to-all-start
  406.0 6.4 all-to-all-start.1
  412.5 6.5 all-to-all-done.1
  422.1 6.2 all_to_all.90
  432.6 6.3 all-to-all-done.3
  440.8 4.1 fusion.16
  454.4 6.2 all_to_all.91
  473.2 6.4 all-to-all-done.5
  481.6 38.4 %all-reduce.3 = (f32[]{:T(128)}, f32[]{:T(128)}) all-reduce(f32[]{:T(128)} %get-tuple-element.41, f32[]{:T(128)} %get-tuple-element.40), channel_id=1, replica_groups=mesh['gx'=2,'gy'=16] {'gx','gy'}, use_global_device_ids=true, to_apply=%region_5.6 | all-reduce | flops 2 | bytes 16 | tf_op jit(solution)/shard_map/psum | solution.py:199
  522.7 7.4 all_to_all.92
  534.3 6.4 all-to-all-done.7
  556.5 6.2 all_to_all.93
  575.3 6.4 all-to-all-done.9
  583.7 38.3 %all-reduce.2 = (f32[]{:T(128)}, f32[]{:T(128)}) all-reduce(f32[]{:T(128)} %get-tuple-element.39, f32[]{:T(128)} %get-tuple-element.38), channel_id=1, replica_groups=mesh['gx'=2,'gy'=16] {'gx','gy'}, use_global_device_ids=true, to_apply=%region_13.14 | all-reduce | flops 2 | bytes 16 | tf_op jit(solution)/shard_map/psum | solution.py:199
  627.9 7.4 all_to_all.94
  639.6 6.4 all-to-all-done.11
  647.9 4.1 fusion.12
  661.5 6.2 all_to_all.95
  680.4 6.4 all-to-all-done.13
  688.8 38.4 %all-reduce.1 = (f32[]{:T(128)}, f32[]{:T(128)}) all-reduce(f32[]{:T(128)} %get-tuple-element.37, f32[]{:T(128)} %get-tuple-element.36), channel_id=1, replica_groups=mesh['gx'=2,'gy'=16] {'gx','gy'}, use_global_device_ids=true, to_apply=%region_21.22 | all-reduce | flops 2 | bytes 16 | tf_op jit(solution)/shard_map/psum | solution.py:199
  732.5 7.4 all_to_all.96
  744.2 6.4 all-to-all-done.15
  752.5 4.1 fusion.18
  766.2 6.2 all_to_all.97
  785.0 6.4 all-to-all-done.17
  793.5 38.4 %all-reduce = (f32[]{:T(128)}, f32[]{:T(128)}) all-reduce(f32[]{:T(128)} %get-tuple-element.35, f32[]{:T(128)} %get-tuple-element.34), channel_id=1, replica_groups=mesh['gx'=2,'gy'=16] {'gx','gy'}, use_global_device_ids=true, to_apply=%region_29.30 | all-reduce | flops 2 | bytes 16 | tf_op jit(solution)/shard_map/psum | solution.py:199
  (311 shorter events, 169.5 us)
Async XLA Ops:
  0.6 0.7 copy-start
  11.1 2.8 copy-start.2
  354.2 5.9 slice-start
  361.2 5.6 copy-start.4
  361.2 5.9 copy-start.3
  361.2 5.9 copy-start.5
  370.9 2.7 copy-start.1
  370.9 2.6 copy-start.6
  384.2 10.8 %copy-start.8 = (s32[1,2,4]{2,1,0:T(2,128)S(1)}, s32[1,2,4]{2,1,0:T(2,128)}, u32[]{:S(2)}) copy-start(s32[1,2,4]{2,1,0:T(2,128)} %param.15) | copy-start | bytes 100
  384.2 10.9 %copy-start.7 = (s32[1,2,4]{2,1,0:T(2,128)S(1)}, s32[1,2,4]{2,1,0:T(2,128)}, u32[]{:S(2)}) copy-start(s32[1,2,4]{2,1,0:T(2,128)} %param.16) | copy-start | bytes 100
  384.2 11.8 %copy-start.9 = (s32[1,2]{1,0:T(1,128)S(1)}, s32[1,2]{1,0:T(1,128)}, u32[]{:S(2)}) copy-start(s32[1,2]{1,0:T(1,128)} %param.18) | copy-start | bytes 28
  384.2 17.2 %copy-start.10 = (s32[1,2]{1,0:T(1,128)S(1)}, s32[1,2]{1,0:T(1,128)}, u32[]{:S(2)}) copy-start(s32[1,2]{1,0:T(1,128)} %param.17) | copy-start | bytes 28
  397.2 8.2 all-to-all-start
  406.0 13.0 %all-to-all-start.1 = ((f32[2,16,200]{2,0,1:T(2,128)}), f32[2,16,200]{2,0,1:T(2,128)S(1)}, u32[]{:S(2)}, u32[]{:S(2)}) async-start(f32[2,16,200]{2,0,1:T(2,128)} %copy.730), calls=%async_computation.1 | async-start | bytes 65536 | tf_op jit(solution)/shard_map/all_to_all | solution.py:169
  428.9 10.0 %all-to-all-start.3 = ((f32[2,16,100]{2,0,1:T(2,128)}), f32[2,16,100]{2,0,1:T(2,128)S(1)}, u32[]{:S(2)}, u32[]{:S(2)}) async-start(f32[2,16,100]{2,0,1:T(2,128)} %copy.738), calls=%async_computation.3 | async-start | bytes 32768 | tf_op jit(solution)/shard_map/all_to_all | solution.py:179
  469.6 10.0 %all-to-all-start.5 = ((f32[16,2,1,100]{3,1,2,0:T(2,128)}), f32[16,2,1,100]{3,1,2,0:T(2,128)S(1)}, u32[]{:S(2)}, u32[]{:S(2)}) async-start(f32[16,2,1,100]{3,1,2,0:T(2,128)} %constant_dynamic-update-slice_fusion), calls=%async_computation.5 | async-start | bytes 32768 | tf_op jit(solution)/shard_map/all_to_all | solution.py:191
  530.7 10.1 %all-to-all-start.7 = ((f32[2,16,100]{2,0,1:T(2,128)}), f32[2,16,100]{2,0,1:T(2,128)S(1)}, u32[]{:S(2)}, u32[]{:S(2)}) async-start(f32[2,16,100]{2,0,1:T(2,128)} %copy.766), calls=%async_computation.7 | async-start | bytes 32768 | tf_op jit(solution)/shard_map/all_to_all | solution.py:179
  571.7 10.0 %all-to-all-start.9 = ((f32[16,2,1,100]{3,1,2,0:T(2,128)}), f32[16,2,1,100]{3,1,2,0:T(2,128)S(1)}, u32[]{:S(2)}, u32[]{:S(2)}) async-start(f32[16,2,1,100]{3,1,2,0:T(2,128)} %constant_dynamic-update-slice_fusion.16), calls=%async_computation.9 | async-start | bytes 32768 | tf_op jit(solution)/shard_map/all_to_all | solution.py:191
  636.0 10.0 %all-to-all-start.11 = ((f32[2,16,100]{2,0,1:T(2,128)}), f32[2,16,100]{2,0,1:T(2,128)S(1)}, u32[]{:S(2)}, u32[]{:S(2)}) async-start(f32[2,16,100]{2,0,1:T(2,128)} %copy.794), calls=%async_computation.11 | async-start | bytes 32768 | tf_op jit(solution)/shard_map/all_to_all | solution.py:179
  676.8 10.0 %all-to-all-start.13 = ((f32[16,2,1,100]{3,1,2,0:T(2,128)}), f32[16,2,1,100]{3,1,2,0:T(2,128)S(1)}, u32[]{:S(2)}, u32[]{:S(2)}) async-start(f32[16,2,1,100]{3,1,2,0:T(2,128)} %constant_dynamic-update-slice_fusion.32), calls=%async_computation.13 | async-start | bytes 32768 | tf_op jit(solution)/shard_map/all_to_all | solution.py:191
  740.5 10.1 %all-to-all-start.15 = ((f32[2,16,100]{2,0,1:T(2,128)}), f32[2,16,100]{2,0,1:T(2,128)S(1)}, u32[]{:S(2)}, u32[]{:S(2)}) async-start(f32[2,16,100]{2,0,1:T(2,128)} %copy.822), calls=%async_computation.15 | async-start | bytes 32768 | tf_op jit(solution)/shard_map/all_to_all | solution.py:179
  781.4 10.0 %all-to-all-start.17 = ((f32[16,2,1,100]{3,1,2,0:T(2,128)}), f32[16,2,1,100]{3,1,2,0:T(2,128)S(1)}, u32[]{:S(2)}, u32[]{:S(2)}) async-start(f32[16,2,1,100]{3,1,2,0:T(2,128)} %constant_dynamic-update-slice_fusion.48), calls=%async_computation.17 | async-start | bytes 32768 | tf_op jit(solution)/shard_map/all_to_all | solution.py:191
